TPU v7x, 32 devices: a whole 2x2x4 slice. The times are simulated.
32 devices in a mesh: wide: 8 (over y, x, core), narrow: 4 (over z).
Axes of the slice: x: 2, y: 2, z: 4, core: 2. Of those that a mesh axis runs over, the one named last changes fastest.
Arguments:
- first_state: float32 [2, 32768, 1024], P(None, ('wide', 'narrow')), may hold values from -100 to 100
- second_state: float32 [2, 32768, 1024], P(None, ('wide', 'narrow')), may hold values from -200 to 200
- place_first: int32 [32768], replicated, may hold values from 0 to 32767, as said below
- place_second: int32 [32768], replicated, may hold values from 0 to 32767, as said below
Outputs:
- aligned: float32 [2, 32768, 1024], P(None, ('wide', 'narrow'))
- intersection: float32 [2], replicated
- norms: float32 [2], replicated
Inputs may be any that keep to these rules, and one draw needn't show every extreme that they name: Each of place_first and place_second maps a logical block index to a storage block index by a permutation of the index's bits. Every logical bit that selects a device (the high bits of a storage index above its position within a device) in one state's order selects a block within a device in the other's, so each device holds exactly 32 blocks of the second state that the first state's order places on any given device. `place_second`: drawn together with place_first under the rule stated there.
All inputs are finite; a program needn't handle non-finite values.
Results may differ from a plain program's by a relative error of at most 0.00002.
Values sent between devices are 32-bit elements; how exact they have to be, the bound alone decides.
A program may use at most 128 MiB of HBM per device.

v0:
```python
import jax
import jax.numpy as jnp
from jax import lax
from jax.sharding import PartitionSpec as P


def bit_index(value, block_bits):
    found = jnp.zeros((), jnp.int32)
    for shift_pos in range(block_bits):
        found = found + (jnp.right_shift(value, shift_pos) & 1) * shift_pos
    return found


def logical_from(store, place, block_bits):
    logical = jnp.zeros_like(store)
    for level in range(block_bits):
        spot = bit_index(place[1 << level], block_bits)
        logical = logical + jnp.left_shift(jnp.right_shift(store, spot) & 1, level)
    return logical


def local(first_state, second_state, place_first, place_second):
    blocks_dev = first_state.shape[1]
    block = first_state.shape[2]
    wide_count = lax.axis_size("wide")
    narrow_count = lax.axis_size("narrow")
    devices = wide_count * narrow_count
    share = blocks_dev // devices
    block_bits = (blocks_dev * devices).bit_length() - 1
    own_index = lax.axis_index("wide") * narrow_count + lax.axis_index("narrow")
    local_slots = jnp.arange(blocks_dev, dtype=jnp.int32)
    own_store = own_index * blocks_dev + local_slots
    target = place_first[logical_from(own_store, place_second, block_bits)]
    send_order = jnp.argsort(target)
    outgoing = jnp.take(second_state, send_order, axis=1)
    first_sq = jnp.sum(first_state * first_state)
    second_sq = jnp.sum(second_state * second_state)
    direct = outgoing.reshape(2, devices, share, block)
    arrived = lax.all_to_all(direct, ("wide", "narrow"), split_axis=1, concat_axis=1, tiled=True)
    arrived = arrived.reshape(2, blocks_dev, block)
    anchor = place_second[logical_from(own_store, place_first, block_bits)]
    source_device = anchor // blocks_dev
    arrival_order = jnp.argsort(source_device * blocks_dev + local_slots)
    gathered = jnp.take(arrived, jnp.argsort(arrival_order), axis=1)
    real_part = jnp.sum(first_state[0] * gathered[0] + first_state[1] * gathered[1])
    imag_part = jnp.sum(first_state[0] * gathered[1] - first_state[1] * gathered[0])
    totals = lax.psum((first_sq, second_sq, real_part, imag_part), ("wide", "narrow"))
    amp_total = float(blocks_dev * devices * block)
    mean_first = totals[0] / amp_total
    mean_second = totals[1] / amp_total
    aligned = gathered / jnp.sqrt(mean_second + 1e-06)
    intersection = (
        jnp.stack([totals[2], totals[3]])
        / amp_total
        / jnp.sqrt((mean_first + 1e-06) * (mean_second + 1e-06))
    )
    norms = jnp.stack([mean_first, mean_second])
    return (aligned, intersection, norms)


def solution(mesh):
    return jax.shard_map(
        local,
        mesh=mesh,
        in_specs=(P(None, ("wide", "narrow"), None), P(None, ("wide", "narrow"), None), P(), P()),
        out_specs=(P(None, ("wide", "narrow"), None), P(), P()),
        check_vma=False,
    )
```

profile of v0, /device:TPU:0, one launch (start us, length us, event | category | flops | bytes accessed | tf_op | source)
XLA Modules:
  0.0 507.3 jit_solution(1075140396495126369)
XLA Ops:
  0.6 1.8 fusion.9
  136.0 0.1 compare_select_fusion.1
  136.1 5.9 %gather_fusion = s32[1024]{0:T(1024)S(1)} fusion(s32[32768]{0:T(1024)} %param.8, s32[1024]{0:T(1024)S(1)} %broadcast_clamp_fusion), kind=kCustom, calls=%fused_computation.2 | custom fusion | bytes 12288 | tf_op jit(solution)/shard_map/gather | solution.py:33
  142.0 4.4 sort.45
  146.4 27.4 %gather_fusion.2 = f32[1024,2,1024]{2,0,1:T(8,128)} fusion(f32[2,1024,1024]{2,1,0:T(8,128)} %param.7, s32[1024]{0:T(1024)S(1)} %fusion.4), kind=kCustom, calls=%fused_computation.clone | custom fusion | bytes 16781312 | tf_op jit(solution)/shard_map/jit(_take)/gather | solution.py:35
  173.8 4.0 broadcast_select_fusion
  177.8 4.2 copy.11
  182.1 0.0 copy-start
  182.1 7.6 %all-to-all-start = ((f32[2,32,32,1024]{3,2,0,1:T(8,128)}), f32[2,32,32,1024]{3,2,0,1:T(8,128)}, u32[]{:S(2)}, u32[]{:S(2)}) async-start(f32[2,32,32,1024]{3,2,0,1:T(8,128)} %copy.11), calls=%async_computation | async-start | bytes 16777216 | tf_op jit(solution)/shard_map/all_to_all | solution.py:39
  189.7 1.7 fusion.8
  323.6 0.1 compare_select_fusion
  323.7 0.0 copy-done
  323.7 6.2 %gather_fusion.1 = s32[1024]{0:T(1024)S(1)} fusion(s32[32768]{0:T(1024)S(1)} %copy-done, s32[1024]{0:T(1024)S(1)} %broadcast_clamp_fusion.1), kind=kCustom, calls=%fused_computation.3 | custom fusion | bytes 12288 | tf_op jit(solution)/shard_map/gather | solution.py:41
  329.9 4.4 sort.46
  334.3 4.4 sort.47
  338.7 8.3 %fusion.7 = (f32[1,1024,1024]{2,1,0:T(8,128)}, f32[1,1024,1024]{2,1,0:T(8,128)}) fusion(f32[2,1024,1024]{2,1,0:T(8,128)} %param.6), kind=kLoop, calls=%fused_computation.34 | loop fusion | bytes 16777216 | tf_op jit(solution)/shard_map/slice | solution.py:45
  347.0 8.5 %multiply_reduce_fusion = (f32[]{:T(128)}, f32[]{:T(128)}) fusion(f32[2,1024,1024]{2,1,0:T(8,128)} %param.6, f32[2,1024,1024]{2,1,0:T(8,128)} %param.7), kind=kLoop, calls=%fused_computation.5 | loop fusion | flops 8388606 | bytes 16777224 | tf_op jit(solution)/shard_map/reduce_sum | solution.py:36
  355.5 15.4 %all-to-all-done = f32[2,32,32,1024]{3,2,0,1:T(8,128)} async-done(((f32[2,32,32,1024]{3,2,0,1:T(8,128)}), f32[2,32,32,1024]{3,2,0,1:T(8,128)}, u32[]{:S(2)}, u32[]{:S(2)}) %all-to-all-start) | async-done | bytes 8388640 | tf_op jit(solution)/shard_map/all_to_all | solution.py:39
  370.9 15.3 %copy.12 = f32[2,32,32,1024]{3,0,2,1:T(2,128)} copy(f32[2,32,32,1024]{3,2,0,1:T(8,128)} %all-to-all-done) | data formatting | bytes 16777216 | tf_op jit(solution)/shard_map/all_to_all | solution.py:39
  386.2 20.7 %gather_fusion.3 = f32[1024,2,1024]{2,1,0:T(2,128)} fusion(f32[2,1024,1024]{2,0,1:T(2,128)} %bitcast.44, s32[1024]{0:T(1024)S(1)} %fusion.5), kind=kCustom, calls=%fused_computation.1.clone | custom fusion | bytes 16781312 | tf_op jit(solution)/shard_map/jit(_take)/gather | solution.py:44
  406.9 0.0 copy-start.1
  406.9 0.0 copy-start.2
  406.9 8.3 %select_bitcast_fusion = f32[2,1024,1024]{2,0,1:T(2,128)S(1)} fusion(f32[1024,2,1024]{2,1,0:T(2,128)} %gather_fusion.3, pred[1024]{0:T(1024)(128)(4,1)S(1)} %compare_and_fusion), kind=kLoop, calls=%fused_computation.4 | loop fusion | flops 2097152 | bytes 16778240 | tf_op jit(solution)/shard_map/jit(_take)/select_n | solution.py:44
  415.2 0.0 copy-done.1
  415.2 0.0 copy-done.2
  415.3 30.0 %add_reduce_fusion = (f32[]{:T(128)}, f32[]{:T(128)}) fusion(f32[2,1024,1024]{2,0,1:T(2,128)S(1)} %select_bitcast_fusion, f32[1,1024,1024]{2,1,0:T(8,128)S(1)} %copy-done.2, f32[1,1024,1024]{2,1,0:T(8,128)S(1)} %copy-done.1), kind=kLoop, calls=%fused_computation.9 | loop fusion | flops 8388606 | bytes 16777224 | tf_op jit(solution)/shard_map/reduce_sum | solution.py:45
  445.2 45.1 %all-reduce = (f32[]{:T(128)}, f32[1]{0:T(128)}, f32[1]{0:T(128)}, f32[]{:T(128)}) all-reduce(f32[]{:T(128)} %get-tuple-element.55, f32[1]{0:T(128)} %bitcast.37, f32[1]{0:T(128)} %bitcast.36, f32[]{:T(128)} %get-tuple-element.54), channel_id=1, replica_groups=mesh['wide'=8,'narrow'=4] {'wide','narrow'}, use_global_device_ids=true, to_apply=%region_4.6 | all-reduce | flops 4 | bytes 32 | tf_op jit(solution)/shard_map/psum | solution.py:47
  491.8 7.2 %broadcast_divide_fusion = f32[2,1024,1024]{2,0,1:T(2,128)S(1)} fusion(f32[]{:T(128)S(6)} %sqrt.6, f32[1024,2,1024]{2,1,0:T(2,128)} %gather_fusion.3, pred[1024]{0:T(1024)(128)(4,1)S(1)} %compare_and_fusion), kind=kLoop, calls=%fused_computation.10 | loop fusion | flops 4194304 | bytes 16778244 | tf_op jit(solution)/shard_map/div | solution.py:51
  498.9 6.0 %copy.15 = f32[2,1024,1024]{2,1,0:T(8,128)} copy(f32[2,1024,1024]{2,0,1:T(2,128)S(1)} %broadcast_divide_fusion) | data formatting | bytes 16777216
  504.9 0.6 pad_maximum_fusion
  505.5 1.8 fusion.6
  (10 shorter events, 0.1 us)
Async XLA Ops:
  182.1 141.7 %copy-start = (s32[32768]{0:T(1024)S(1)}, s32[32768]{0:T(1024)}, u32[]{:S(2)}) copy-start(s32[32768]{0:T(1024)} %param.9) | copy-start | bytes 393220
  182.1 188.8 %all-to-all-start = ((f32[2,32,32,1024]{3,2,0,1:T(8,128)}), f32[2,32,32,1024]{3,2,0,1:T(8,128)}, u32[]{:S(2)}, u32[]{:S(2)}) async-start(f32[2,32,32,1024]{3,2,0,1:T(8,128)} %copy.11), calls=%async_computation | async-start | bytes 16777216 | tf_op jit(solution)/shard_map/all_to_all | solution.py:39
  406.9 8.3 %copy-start.1 = (f32[1,1024,1024]{2,1,0:T(8,128)S(1)}, f32[1,1024,1024]{2,1,0:T(8,128)}, u32[]{:S(2)}) copy-start(f32[1,1024,1024]{2,1,0:T(8,128)} %get-tuple-element.22) | copy-start | bytes 12582916
  406.9 8.4 %copy-start.2 = (f32[1,1024,1024]{2,1,0:T(8,128)S(1)}, f32[1,1024,1024]{2,1,0:T(8,128)}, u32[]{:S(2)}) copy-start(f32[1,1024,1024]{2,1,0:T(8,128)} %get-tuple-element.23) | copy-start | bytes 12582916
where the time goes:
time: 512 us; the launch traced here: 507 us
  between operations  268 us (52%)
  local copies, waits for them, and re-layouts  97.6 us (19%)
  other arithmetic  73.7 us (14%)
  blocking collectives  45.1 us (9%)
  waiting for transfers between devices  15.4 us (3%)
  starting transfers between devices  7.63 us (1%)
    psum x1, blocking collectives, local(): lax.psum((first_sq, second_sq, real_part, imag_part), ('wide', 'narrow'))  45.1 us
    reduce_sum x1, other arithmetic, local(): jnp.sum(first_state[0] * gathered[0] + first_state[1] * gathered[1])  30 us
    gather x1, local copies, waits for them, and re-layouts, local(): outgoing = jnp.take(second_state, send_order, axis=1)  27.4 us
    gather x1, local copies, waits for them, and re-layouts, local(): gathered = jnp.take(arrived, jnp.argsort(arrival_order), axis=1)  20.7 us
    all_to_all x1, waiting for transfers between devices, local(): lax.all_to_all(direct, ('wide', 'narrow'), split_axis=1, concat_axis=1, t...  15.4 us
    all_to_all x1, local copies, waits for them, and re-layouts, local(): lax.all_to_all(direct, ('wide', 'narrow'), split_axis=1, concat_axis=1, t...  15.3 us
  transfers between devices with their start and end apart: 1, of which 1 were waited for; matrix products, arithmetic and copies ran while one was open for 7% of the time, Pallas kernels for 0%

commit v1 on v0

v1 whole, which is shorter than its diff:
```python
import functools

import jax
import jax.numpy as jnp
from jax import lax
from jax.experimental import pallas as pl
from jax.experimental.pallas import tpu as pltpu
from jax.sharding import PartitionSpec as P

MESH = pl.DeviceIdType.MESH
SUB = 8
LANE = 128


def bit_places(place, levels):
    powers = jnp.stack([place[1 << level] for level in range(levels)])
    found = jnp.zeros_like(powers)
    for spot in range(levels):
        found = found + (jnp.right_shift(powers, spot) & 1) * spot
    return found


def maps(place_first, place_second, blocks_dev, devices):
    levels = (blocks_dev * devices).bit_length() - 1
    local_bits = blocks_dev.bit_length() - 1
    share_bits = (blocks_dev // devices).bit_length() - 1
    pf = bit_places(place_first, levels)
    ps = bit_places(place_second, levels)
    f_local = pf < local_bits
    s_local = ps < local_bits
    both = (f_local & s_local).astype(jnp.int32)
    rank = jnp.cumsum(both) - both
    out_pos = jnp.where(f_local, rank, pf - local_bits + share_bits)
    in_pos = jnp.where(s_local, rank, ps - local_bits + share_bits)
    t = jnp.arange(blocks_dev, dtype=jnp.int32)
    send = jnp.zeros_like(t)
    land = jnp.zeros_like(t)
    back = jnp.zeros_like(t)
    for level in range(levels):
        send += jnp.where(s_local[level], ((t >> out_pos[level]) & 1) << jnp.where(s_local[level], ps[level], 0), 0)
        land += jnp.where(f_local[level], ((t >> in_pos[level]) & 1) << jnp.where(f_local[level], pf[level], 0), 0)
        back += jnp.where(f_local[level], ((t >> jnp.where(f_local[level], pf[level], 0)) & 1) << in_pos[level], 0)
    return send, land, back


def row_of(part, slot, blocks_dev):
    return part * (blocks_dev * SUB) + (slot // SUB) * (SUB * SUB) + lax.rem(slot, SUB)


def exchange(sizes, blocks_dev, share, send_map, land_map, first_hbm, second_hbm, recv_hbm, stats_out,
             first, second, outgoing, arrived, stats, totals,
             load_sem, send_sem, recv_sem, keep_sem, sq_send, sq_recv, dot_send, dot_recv):
    wide_count, narrow_count = sizes
    devices = wide_count * narrow_count
    me_w = lax.axis_index("wide")
    me_n = lax.axis_index("narrow")
    me = me_w * narrow_count + me_n

    load_second = pltpu.make_async_copy(second_hbm, second, load_sem.at[0])
    load_first = pltpu.make_async_copy(first_hbm, first, load_sem.at[1])
    load_second.start()
    load_first.start()

    def partner(step):
        other_w = lax.rem(me_w + step // narrow_count, wide_count)
        other_n = lax.rem(me_n + lax.rem(step, narrow_count), narrow_count)
        return other_w, other_n

    def giver(step):
        other_w = lax.rem(me_w + wide_count - step // narrow_count, wide_count)
        other_n = lax.rem(me_n + narrow_count - lax.rem(step, narrow_count), narrow_count)
        return other_w * narrow_count + other_n

    barrier = pltpu.get_barrier_semaphore()

    @pl.loop(1, devices)
    def _(step):
        pl.semaphore_signal(barrier, inc=1, device_id=partner(step), device_id_type=MESH)

    load_second.wait()
    pl.semaphore_wait(barrier, devices - 1)

    def block_copy(step):
        return pltpu.make_async_remote_copy(
            src_ref=outgoing.at[step], dst_ref=arrived.at[step],
            send_sem=send_sem.at[step], recv_sem=recv_sem.at[step],
            device_id=partner(step), device_id_type=MESH)

    def pack(step):
        other_w, other_n = partner(step)
        base = (other_w * narrow_count + other_n) * share

        def row(k, carry):
            slot = send_map[base + k]
            for part in range(2):
                start = row_of(part, slot, blocks_dev)
                outgoing[step, part, k] = second[pl.ds(start, SUB, stride=SUB), :]
            return carry

        lax.fori_loop(0, share, row, 0, unroll=min(8, share))

    pack(1)

    @pl.loop(2, devices)
    def _(step):
        pack(step)
        block_copy(step - 1).start()

    own_base = me * share

    def own_row(k, carry):
        slot = send_map[own_base + k]
        for part in range(2):
            start = row_of(part, slot, blocks_dev)
            arrived[0, part, k] = second[pl.ds(start, SUB, stride=SUB), :]
        return carry

    lax.fori_loop(0, share, own_row, 0, unroll=min(8, share))
    block_copy(devices - 1).start()

    load_first.wait()
    rows = 2 * blocks_dev * SUB
    chunk = 16 * SUB

    def squares(i, carry):
        at = pl.multiple_of(i * chunk, chunk)
        a = first[pl.ds(at, chunk), :].reshape(chunk // SUB, SUB, LANE)
        b = second[pl.ds(at, chunk), :].reshape(chunk // SUB, SUB, LANE)
        return carry[0] + jnp.sum(a * a, axis=0), carry[1] + jnp.sum(b * b, axis=0)

    zero = jnp.zeros((SUB, LANE), jnp.float32)
    sq_first, sq_second = lax.fori_loop(0, rows // chunk, squares, (zero, zero))
    stats[0, 0] = jnp.broadcast_to(jnp.sum(sq_first, axis=0, keepdims=True), (SUB, LANE))
    stats[0, 1] = jnp.broadcast_to(jnp.sum(sq_second, axis=0, keepdims=True), (SUB, LANE))

    def keep(step):
        return pltpu.make_async_copy(arrived.at[step], recv_hbm.at[giver(step)], keep_sem.at[step])

    def dots(step, carry):
        base = giver(step) * share

        def row(k, carry):
            real, imag = carry
            slot = land_map[base + k]
            f_re = first[pl.ds(row_of(0, slot, blocks_dev), SUB, stride=SUB), :]
            f_im = first[pl.ds(row_of(1, slot, blocks_dev), SUB, stride=SUB), :]
            g_re = arrived[step, 0, k]
            g_im = arrived[step, 1, k]
            return real + (f_re * g_re + f_im * g_im), imag + (f_re * g_im - f_im * g_re)

        return lax.fori_loop(0, share, row, carry, unroll=min(8, share))

    keep(0).start()
    carry = dots(0, (zero, zero))

    def sq_copy(step):
        return pltpu.make_async_remote_copy(
            src_ref=stats.at[0], dst_ref=totals.at[0, step],
            send_sem=sq_send.at[step], recv_sem=sq_recv.at[step],
            device_id=partner(step), device_id_type=MESH)

    def dot_copy(step):
        return pltpu.make_async_remote_copy(
            src_ref=stats.at[1], dst_ref=totals.at[1, step],
            send_sem=dot_send.at[step], recv_sem=dot_recv.at[step],
            device_id=partner(step), device_id_type=MESH)

    @pl.loop(1, devices)
    def _(step):
        sq_copy(step).start()

    def take(step, carry):
        block_copy(step).wait_recv()
        keep(step).start()
        return dots(step, carry)

    real, imag = lax.fori_loop(1, devices, take, carry)
    stats[1, 0] = jnp.broadcast_to(jnp.sum(real, axis=0, keepdims=True), (SUB, LANE))
    stats[1, 1] = jnp.broadcast_to(jnp.sum(imag, axis=0, keepdims=True), (SUB, LANE))

    @pl.loop(1, devices)
    def _(step):
        block_copy(step).wait_send()
        sq_copy(step).wait()
        keep(step).wait()

    @pl.loop(1, devices)
    def _(step):
        dot_copy(step).start()

    keep(0).wait()
    totals[0, 0] = stats[0]
    totals[1, 0] = stats[1]

    @pl.loop(1, devices)
    def _(step):
        dot_copy(step).wait()

    def add(device, carry):
        gone_w = lax.rem(me_w + wide_count - device // narrow_count, wide_count)
        gone_n = lax.rem(me_n + narrow_count - lax.rem(device, narrow_count), narrow_count)
        step = gone_w * narrow_count + gone_n
        return carry + totals[:, step]

    stats_out[...] = lax.fori_loop(0, devices, add, jnp.zeros((2, 2, SUB, LANE), jnp.float32))


def unpack(blocks_dev, groups, back_map, scale, recv_hbm, out, arrived, sem):
    at = pl.program_id(0)

    @pl.when(at == 0)
    def _():
        copy = pltpu.make_async_copy(recv_hbm, arrived, sem)
        copy.start()
        copy.wait()

    share = arrived.shape[2]
    factor = scale[0]

    def group(i, carry):
        base = pl.multiple_of(i * (SUB * SUB), SUB * SUB)
        for r in range(SUB):
            index = back_map[(at * groups + i) * SUB + r]
            device = index // share
            k = lax.rem(index, share)
            for part in range(2):
                out[part, pl.ds(base + r, SUB, stride=SUB), :] = arrived[device, part, k] * factor
        return carry

    lax.fori_loop(0, groups, group, 0)


def local(first_state, second_state, place_first, place_second):
    blocks_dev = first_state.shape[1]
    block = first_state.shape[2]
    wide_count = lax.axis_size("wide")
    narrow_count = lax.axis_size("narrow")
    devices = wide_count * narrow_count
    share = blocks_dev // devices
    send_map, land_map, back_map = maps(place_first, place_second, blocks_dev, devices)

    def tiles(state):
        split = state.reshape(2, blocks_dev // SUB, SUB, block // LANE, LANE)
        return split.transpose(0, 1, 3, 2, 4).reshape(2 * blocks_dev * SUB, LANE)

    packed = (devices, 2, share, SUB, LANE)
    recv, totals = pl.pallas_call(
        functools.partial(exchange, (wide_count, narrow_count), blocks_dev, share),
        out_shape=(jax.ShapeDtypeStruct(packed, jnp.float32),
                   jax.ShapeDtypeStruct((2, 2, SUB, LANE), jnp.float32)),
        in_specs=[pl.BlockSpec(memory_space=pltpu.SMEM)] * 2 + [pl.BlockSpec(memory_space=pl.ANY)] * 2,
        out_specs=(pl.BlockSpec(memory_space=pl.ANY), pl.BlockSpec(memory_space=pltpu.VMEM)),
        scratch_shapes=[
            pltpu.VMEM((2 * blocks_dev * SUB, LANE), jnp.float32),
            pltpu.VMEM((2 * blocks_dev * SUB, LANE), jnp.float32),
            pltpu.VMEM(packed, jnp.float32),
            pltpu.VMEM(packed, jnp.float32),
            pltpu.VMEM((2, 2, SUB, LANE), jnp.float32),
            pltpu.VMEM((2, devices, 2, SUB, LANE), jnp.float32),
            pltpu.SemaphoreType.DMA((2,)),
        ] + [pltpu.SemaphoreType.DMA((devices,))] * 7,
        compiler_params=pltpu.CompilerParams(
            collective_id=0, has_side_effects=True, vmem_limit_bytes=48 * 1024 * 1024),
        name="exchange",
    )(send_map, land_map, tiles(first_state), tiles(second_state))

    amp_total = float(blocks_dev * devices * block)
    sums = jnp.sum(totals[:, :, 0, :], axis=-1) / amp_total
    mean_first = sums[0, 0]
    mean_second = sums[0, 1]
    scale = 1.0 / jnp.sqrt(mean_second + 1e-06)
    steps = 8
    groups = blocks_dev // SUB // steps
    aligned = pl.pallas_call(
        functools.partial(unpack, blocks_dev, groups),
        out_shape=jax.ShapeDtypeStruct((2, blocks_dev * SUB, LANE), jnp.float32),
        grid=(steps,),
        in_specs=[pl.BlockSpec(memory_space=pltpu.SMEM)] * 2 + [pl.BlockSpec(memory_space=pl.ANY)],
        out_specs=pl.BlockSpec((2, groups * SUB * SUB, LANE), lambda i: (0, i, 0)),
        scratch_shapes=[pltpu.VMEM(packed, jnp.float32), pltpu.SemaphoreType.DMA],
        name="unpack",
    )(back_map, scale.reshape(1), recv)
    aligned = aligned.reshape(2, blocks_dev // SUB, block // LANE, SUB, LANE)
    aligned = aligned.transpose(0, 1, 3, 2, 4).reshape(2, blocks_dev, block)
    intersection = sums[1] / jnp.sqrt((mean_first + 1e-06) * (mean_second + 1e-06))
    norms = jnp.stack([mean_first, mean_second])
    return (aligned, intersection, norms)


def solution(mesh):
    return jax.shard_map(
        local,
        mesh=mesh,
        in_specs=(P(None, ("wide", "narrow"), None), P(None, ("wide", "narrow"), None), P(), P()),
        out_specs=(P(None, ("wide", "narrow"), None), P(), P()),
        check_vma=False,
    )
```

time: 512 us -> 363 us (0.71)
  between operations: 268 us -> 39.6 us
  Pallas kernels: 0 us -> 219 us
  local copies, waits for them, and re-layouts: 97.6 us -> 43 us
  blocking collectives: 45.1 us -> 0 us
  waiting for transfers between devices: 15.4 us -> 0 us
  other arithmetic: 73.7 us -> 59.1 us
  starting transfers between devices: 7.63 us -> 0 us
    pallas_call x0 -> x2, Pallas kernels: none -> 219 us  [the longest x1 207 us: local(): pl.pallas_call(functools.partial(exchange, (wide_count, narrow_count), bl...]
    gather x4 -> x0, local copies, waits for them, and re-layouts: 60.2 us -> none  [the longest x1 27.4 us: local(): outgoing = jnp.take(second_state, send_order, axis=1)]
    add x1 -> x3, other arithmetic: 0.01 us -> 56.4 us  [the longest x1 19.1 us: maps(): back += jnp.where(f_local[level], (t >> jnp.where(f_local[level], pf[leve...]
    psum x1 -> x0, blocking collectives: 45.1 us -> none  [local(): lax.psum((first_sq, second_sq, real_part, imag_part), ('wide', 'narrow'))]
    reduce_sum x2 -> x1, other arithmetic: 38.5 us -> 0.1 us  [local(): sums = jnp.sum(totals[:, :, 0, :], axis=-1) / amp_total]
    another operation x0 -> x4, local copies, waits for them, and re-layouts: none -> 33.2 us  [bit_places(): powers = jnp.stack([place[1 << level] for level in range(levels)])]
    all_to_all x1 -> x0, waiting for transfers between devices: 15.4 us -> none  [local(): lax.all_to_all(direct, ('wide', 'narrow'), split_axis=1, concat_axis=1, t...]
    all_to_all x1 -> x0, local copies, waits for them, and re-layouts: 15.3 us -> none  [local(): lax.all_to_all(direct, ('wide', 'narrow'), split_axis=1, concat_axis=1, t...]
  transfers between devices with their start and end apart: 1 -> 0, of which waited for: 1 -> 0; matrix products, arithmetic and copies ran while one was open for 7% -> 0% of each run, Pallas kernels for 0% -> 0%
where the time goes in v1:
time: 363 us; the launch traced here: 361 us
  Pallas kernels  219 us (60%)
  other arithmetic  59.1 us (16%)
  local copies, waits for them, and re-layouts  43 us (12%)
  between operations  39.6 us (11%)
    pallas_call x1, Pallas kernels, local(): pl.pallas_call(functools.partial(exchange, (wide_count, narrow_count), bl...  207 us
    another operation x4, local copies, waits for them, and re-layouts, bit_places(): powers = jnp.stack([place[1 << level] for level in range(levels)])  33.2 us
    add x1, other arithmetic, maps(): back += jnp.where(f_local[level], (t >> jnp.where(f_local[level], pf[leve...  19.1 us
    add x1, other arithmetic, maps(): send += jnp.where(s_local[level], (t >> out_pos[level] & 1) << jnp.where(...  18.9 us
    add x1, other arithmetic, maps(): land += jnp.where(f_local[level], (t >> in_pos[level] & 1) << jnp.where(f...  18.5 us
    pallas_call x1, Pallas kernels, local(): pl.pallas_call(functools.partial(unpack, blocks_dev, groups), out_shape=j...  12.6 us

profile of v1, /device:TPU:0, one launch (start us, length us, event | category | flops | bytes accessed | tf_op | source)
XLA Modules:
  0.0 361.1 jit_solution(4834745352105059289)
XLA Ops:
  0.6 1.7 fusion.3
  2.3 0.8 fusion.2
  3.1 8.2 %stack.87 = s32[15,1]{0,1:T(1,128)S(1)} concatenate(s32[2,1]{0,1:T(1,128)S(1)} %get-tuple-element.13, s32[1,1]{0,1:T(1,128)} %bitcast.3, s32[1,1]{0,1:T(1,128)} %bitcast.4, s32[1,1]{0,1:T(1,128)} %bitcast.5, s32[1,1]{0,1:T(1,128)} %bitcast.6, s32[1,1]{0,1:T(1,128)} %bitcast.7, s32[1,1]{0,1:T(1,128)} %bitcast.8, s32[1,1]{0,1:T(1,128)} %bitcast.9, s32[1,1]{0,1:T(1,128)} %bitcast.10, ...), dimensions={0} | concatenate | bytes 120 | tf_op jit(solution)/shard_map/stack | solution.py:16
  11.3 1.7 fusion.4
  13.0 0.8 fusion.1
  13.7 8.4 %stack.102 = s32[15,1]{0,1:T(1,128)S(1)} concatenate(s32[2,1]{0,1:T(1,128)S(1)} %get-tuple-element.11, s32[1,1]{0,1:T(1,128)} %bitcast.17, s32[1,1]{0,1:T(1,128)} %bitcast.18, s32[1,1]{0,1:T(1,128)} %bitcast.19, s32[1,1]{0,1:T(1,128)} %bitcast.20, s32[1,1]{0,1:T(1,128)} %bitcast.21, s32[1,1]{0,1:T(1,128)} %bitcast.22, s32[1,1]{0,1:T(1,128)} %bitcast.23, s32[1,1]{0,1:T(1,128)} %bitcast.24, ...), dimensions={0} | concatenate | bytes 120 | tf_op jit(solution)/shard_map/stack | solution.py:16
  22.1 0.2 reduce-window.9
  22.3 8.4 %stack.72 = s32[15]{0:T(128)S(1)} concatenate(s32[2]{0:T(128)S(1)} %get-tuple-element.10, s32[1]{0:T(128)} %get-tuple-element.38, s32[1]{0:T(128)} %get-tuple-element.37, s32[1]{0:T(128)} %get-tuple-element.36, s32[1]{0:T(128)} %get-tuple-element.35, s32[1]{0:T(128)} %get-tuple-element.34, s32[1]{0:T(128)} %get-tuple-element.33, s32[1]{0:T(128)} %get-tuple-element.32, ...), dimensions={0} | concatenate | bytes 120 | tf_op jit(solution)/shard_map/stack | solution.py:16
  30.7 8.2 %stack.71 = s32[15]{0:T(128)S(1)} concatenate(s32[2]{0:T(128)S(1)} %get-tuple-element.12, s32[1]{0:T(128)} %get-tuple-element.25, s32[1]{0:T(128)} %get-tuple-element.24, s32[1]{0:T(128)} %get-tuple-element.23, s32[1]{0:T(128)} %get-tuple-element.22, s32[1]{0:T(128)} %get-tuple-element.21, s32[1]{0:T(128)} %get-tuple-element.20, s32[1]{0:T(128)} %get-tuple-element.19, ...), dimensions={0} | concatenate | bytes 120 | tf_op jit(solution)/shard_map/stack | solution.py:16
  39.0 0.7 fusion.10
  39.7 0.7 fusion.9
  59.1 0.7 fusion.11
  59.8 18.5 %select_add_fusion.land_map = s32[1024]{0:T(1024)S(1)} fusion(s32[]{:T(128)} %bitcast.73, s32[]{:T(128)S(6)} %select_n.399, s32[]{:T(128)} %bitcast.70, s32[]{:T(128)S(6)} %select_n.396, s32[]{:T(128)} %bitcast.67, s32[]{:T(128)S(6)} %select_n.393, s32[]{:T(128)} %bitcast.64, s32[]{:T(128)S(6)} %select_n.390, s32[]{:T(128)} %bitcast.61, s32[]{:T(128)S(6)} %select_n.387, ...), kind=kLoop, calls=%fused_computation | loop fusion | flops 75776 | bytes 4231 | tf_op jit(solution)/shard_map/add | solution.py:41
  78.3 0.7 fusion.8
  79.0 0.7 fusion.7
  98.5 0.7 fusion.6
  99.2 18.9 %select_add_fusion.1.send_map = s32[1024]{0:T(1024)S(1)} fusion(s32[]{:T(128)S(6)} %select_n.445, s32[]{:T(128)} %bitcast.117, s32[]{:T(128)S(6)} %select_n.442, s32[]{:T(128)} %bitcast.114, s32[]{:T(128)S(6)} %select_n.439, s32[]{:T(128)} %bitcast.111, s32[]{:T(128)S(6)} %select_n.436, s32[]{:T(128)} %bitcast.108, s32[]{:T(128)S(6)} %select_n.433, ...), kind=kLoop, calls=%fused_computation.1 | loop fusion | flops 75776 | bytes 4231 | tf_op jit(solution)/shard_map/add | solution.py:40
  118.1 206.8 %exchange.1 = (f32[32,2,32,8,128]{4,3,2,1,0:T(8,128)}, f32[2,2,8,128]{3,2,1,0:T(8,128)S(1)}) custom-call(s32[1024]{0:T(1024)S(1)} %select_add_fusion.1.send_map, s32[1024]{0:T(1024)S(1)} %select_add_fusion.land_map, f32[16384,128]{1,0:T(8,128)} %bitcast.148, f32[16384,128]{1,0:T(8,128)} %bitcast.149), custom_call_target="tpu_custom_call" | custom-call | tf_op jit(solution)/shard_map/exchange/pallas_call | solution.py:247
  324.9 0.1 slice_reduce_fusion
  325.0 0.6 fusion.5
  325.6 1.9 pad_maximum_fusion
  328.8 0.5 divide_bitcast_fusion
  329.4 19.1 %select_add_fusion.2.back_map = s32[1024]{0:T(1024)} fusion(s32[]{:T(128)} %bitcast.73, s32[]{:T(128)S(6)} %select_n.399, s32[]{:T(128)} %bitcast.70, s32[]{:T(128)S(6)} %select_n.396, s32[]{:T(128)} %bitcast.67, s32[]{:T(128)S(6)} %select_n.393, s32[]{:T(128)} %bitcast.64, s32[]{:T(128)S(6)} %select_n.390, s32[]{:T(128)} %bitcast.61, s32[]{:T(128)S(6)} %select_n.387, ...), kind=kLoop, calls=%fused_computation.2 | loop fusion | flops 75776 | bytes 4231 | tf_op jit(solution)/shard_map/add | solution.py:42
  348.4 12.6 %unpack.1 = f32[2,8192,128]{2,1,0:T(8,128)} custom-call(s32[1024]{0:T(1024)} %select_add_fusion.2.back_map, f32[1]{0:T(128)} %bitcast.125.scale, f32[32,2,32,8,128]{4,3,2,1,0:T(8,128)} %get-tuple-element.6.recv_hbm), custom_call_target="tpu_custom_call" | custom-call | tf_op jit(solution)/shard_map/unpack/pallas_call | solution.py:274
  (5 shorter events, 0.1 us)

commit v2 on v0

v2 whole, which is shorter than its diff:
```python
import functools

import jax
import jax.numpy as jnp
from jax import lax
from jax.experimental import pallas as pl
from jax.experimental.pallas import tpu as pltpu
from jax.sharding import PartitionSpec as P

MESH = pl.DeviceIdType.MESH
SUB = 8
LANE = 128


def row_weight(one_hot):
    return jnp.where(one_hot < SUB, one_hot, one_hot * SUB)


def bits(count):
    return count.bit_length() - 1


def table(ref, base, weights):
    ref[base] = jnp.int32(0)
    for level, weight in enumerate(weights):
        for low in range(1 << level):
            ref[base + (1 << level) + low] = ref[base + low] + weight


def build_tables(place_f, place_s, blocks_dev, devices, share, rows_out, rows_in, back):
    levels = bits(blocks_dev * devices)
    zero = jnp.int32(0)
    dev_out = [zero] * bits(devices)
    dev_in = [zero] * bits(devices)
    k_out = [zero] * bits(share)
    k_in = [zero] * bits(share)
    slot_back = [zero] * bits(blocks_dev)
    unit = jnp.int32(1)
    for level in range(levels):
        f = place_f(level)
        s = place_s(level)
        f_dev = f >> bits(blocks_dev)
        s_dev = s >> bits(blocks_dev)
        both = (f_dev == 0) & (s_dev == 0)
        for j in range(bits(devices)):
            dev_out[j] = dev_out[j] + jnp.where(f_dev == (1 << j), row_weight(s), 0)
            dev_in[j] = dev_in[j] + jnp.where(s_dev == (1 << j), row_weight(f), 0)
        for i in range(bits(share)):
            here = both & (unit == (1 << i))
            k_out[i] = k_out[i] + jnp.where(here, row_weight(s), 0)
            k_in[i] = k_in[i] + jnp.where(here, row_weight(f), 0)
        packed = jnp.where(both, unit * SUB, s_dev * (2 * share * SUB))
        for p in range(bits(blocks_dev)):
            slot_back[p] = slot_back[p] + jnp.where(f == (1 << p), packed, 0)
        unit = jnp.where(both, unit * 2, unit)
    table(rows_out, 0, dev_out)
    table(rows_out, devices, k_out)
    table(rows_in, 0, dev_in)
    table(rows_in, devices, k_in)
    table(back, 0, slot_back[:bits(SUB)])
    table(back, SUB, slot_back[bits(SUB):])


def exchange(sizes, blocks_dev, share, place_first, place_second, first_hbm, second_hbm,
             recv_hbm, stats_out, back,
             first, second, outgoing, arrived, stats, totals, powers, rows_out, rows_in,
             load_sem, place_sem, send_sem, recv_sem, keep_sem, sq_send, sq_recv, dot_send, dot_recv):
    wide_count, narrow_count = sizes
    devices = wide_count * narrow_count
    levels = bits(blocks_dev * devices)
    me_w = lax.axis_index("wide")
    me_n = lax.axis_index("narrow")
    me = me_w * narrow_count + me_n
    part_rows = blocks_dev * SUB

    lines = [0] + [1 << line for line in range(levels - bits(LANE))]
    fetches = []
    for which, place in enumerate((place_first, place_second)):
        for at, line in enumerate(lines):
            fetches.append(pltpu.make_async_copy(
                place.at[pl.ds(line, 1), :], powers.at[which, pl.ds(at, 1), :],
                place_sem.at[which * len(lines) + at]))
    load_second = pltpu.make_async_copy(second_hbm, second, load_sem.at[0])
    load_first = pltpu.make_async_copy(first_hbm, first, load_sem.at[1])
    for fetch in fetches:
        fetch.start()
    load_second.start()

    def partner(offset):
        return (jnp.bitwise_xor(me_w, offset // narrow_count),
                jnp.bitwise_xor(me_n, lax.rem(offset, narrow_count)))

    def other(offset):
        other_w, other_n = partner(offset)
        return other_w * narrow_count + other_n

    barrier = pltpu.get_barrier_semaphore()

    @pl.loop(1, devices)
    def _(offset):
        pl.semaphore_signal(barrier, inc=1, device_id=partner(offset), device_id_type=MESH)

    for fetch in fetches:
        fetch.wait()

    def place_of(which):
        def entry(level):
            if (1 << level) < LANE:
                return powers[which, 0, 1 << level]
            return powers[which, 1 + level - bits(LANE), 0]
        return entry

    build_tables(place_of(0), place_of(1), blocks_dev, devices, share, rows_out, rows_in, back)
    load_second.wait()
    load_first.start()
    pl.semaphore_wait(barrier, devices - 1)

    last = narrow_count - 1
    inner = (me_n != 0) & (me_n != last)
    flip = jnp.where(lax.rem(me_w, 2) == 1, wide_count - 2, 0)

    def offset_of(seq):
        turn = seq // wide_count
        far = jnp.where(inner, jnp.where(turn == 0, last, turn), turn + 1)
        away = jnp.bitwise_xor(lax.rem(seq, wide_count), flip) * narrow_count + far
        near = (seq - wide_count * last + 1) * narrow_count
        return jnp.where(turn < last, away, near)

    outside = wide_count * last

    def block_copy(offset):
        return pltpu.make_async_remote_copy(
            src_ref=outgoing.at[offset], dst_ref=arrived.at[offset],
            send_sem=send_sem.at[offset], recv_sem=recv_sem.at[offset],
            device_id=partner(offset), device_id_type=MESH)

    def pack(offset, out):
        base = rows_out[other(offset)]

        def row(k, carry):
            start = base + rows_out[devices + k]
            for part in range(2):
                out[offset, part, k] = second[pl.ds(start + part * part_rows, SUB, stride=SUB), :]
            return carry

        lax.fori_loop(0, share, row, 0, unroll=min(8, share))

    pack(offset_of(0), outgoing)

    @pl.loop(1, devices - 1)
    def _(seq):
        pack(offset_of(seq), outgoing)

        @pl.when(seq <= outside)
        def _():
            block_copy(offset_of(seq - 1)).start()

    pack(0, arrived)

    load_first.wait()
    chunk = 16 * SUB

    def squares(i, carry):
        at = pl.multiple_of(i * chunk, chunk)
        a = first[pl.ds(at, chunk), :].reshape(chunk // SUB, SUB, LANE)
        b = second[pl.ds(at, chunk), :].reshape(chunk // SUB, SUB, LANE)
        return carry[0] + jnp.sum(a * a, axis=0), carry[1] + jnp.sum(b * b, axis=0)

    zero = jnp.zeros((SUB, LANE), jnp.float32)
    sq_first, sq_second = lax.fori_loop(0, 2 * part_rows // chunk, squares, (zero, zero))
    stats[0, 0] = sq_first
    stats[0, 1] = sq_second

    def keep(offset):
        return pltpu.make_async_copy(arrived.at[offset], recv_hbm.at[other(offset)], keep_sem.at[offset])

    def dots(offset, carry):
        base = rows_in[other(offset)]

        def row(k, carry):
            real, imag = carry
            start = base + rows_in[devices + k]
            f_re = first[pl.ds(start, SUB, stride=SUB), :]
            f_im = first[pl.ds(start + part_rows, SUB, stride=SUB), :]
            g_re = arrived[offset, 0, k]
            g_im = arrived[offset, 1, k]
            return real + (f_re * g_re + f_im * g_im), imag + (f_re * g_im - f_im * g_re)

        return lax.fori_loop(0, share, row, carry, unroll=min(8, share))

    keep(0).start()
    carry = dots(0, (zero, zero))

    def sum_copy(kind, sems, offset):
        return pltpu.make_async_remote_copy(
            src_ref=stats.at[kind], dst_ref=totals.at[kind, offset],
            send_sem=sems[0].at[offset], recv_sem=sems[1].at[offset],
            device_id=partner(offset), device_id_type=MESH)

    sq_copy = functools.partial(sum_copy, 0, (sq_send, sq_recv))
    dot_copy = functools.partial(sum_copy, 1, (dot_send, dot_recv))

    @pl.loop(1, devices)
    def _(offset):
        sq_copy(offset).start()

    def take(offset, carry):
        block_copy(offset).wait_recv()
        keep(offset).start()
        return dots(offset, carry)

    def take_and_send(seq, carry):
        block_copy(offset_of(outside + seq)).start()
        return take(offset_of_arrival(seq), carry)

    def offset_of_arrival(seq):
        turn = seq // wide_count
        far = jnp.where(inner, jnp.where(turn == 0, last, turn), turn + 1)
        return jnp.bitwise_xor(lax.rem(seq, wide_count), flip) * narrow_count + far

    carry = lax.fori_loop(0, wide_count - 1, take_and_send, carry)
    carry = take(offset_of_arrival(wide_count - 1), carry)
    carry = lax.fori_loop(outside, devices - 1, lambda seq, c: take(offset_of(seq), c), carry)
    real, imag = lax.fori_loop(
        wide_count, outside, lambda seq, c: take(offset_of_arrival(seq), c), carry)
    stats[1, 0] = real
    stats[1, 1] = imag

    @pl.loop(1, devices)
    def _(offset):
        block_copy(offset).wait_send()
        sq_copy(offset).wait()
        keep(offset).wait()

    @pl.loop(1, devices)
    def _(offset):
        dot_copy(offset).start()

    keep(0).wait()
    totals[0, 0] = stats[0]
    totals[1, 0] = stats[1]

    @pl.loop(1, devices)
    def _(offset):
        dot_copy(offset).wait()

    def add(device, carry):
        return carry + totals[:, jnp.bitwise_xor(me, device)]

    stats_out[...] = lax.fori_loop(0, devices, add, jnp.zeros((2, 2, SUB, LANE), jnp.float32))


def unpack(amp_total, groups, part_rows, back, stats, recv_hbm, out, intersection, norms, arrived, factor, sem):
    at = pl.program_id(0)

    @pl.when(at == 0)
    def _():
        copy = pltpu.make_async_copy(recv_hbm, arrived, sem)
        copy.start()

        def mean(kind, which):
            total = jnp.sum(stats[kind, which]) / amp_total
            return jnp.broadcast_to(total, (SUB, LANE))

        mean_first = mean(0, 0)
        mean_second = mean(0, 1)
        norms[0] = mean_first[0, 0]
        norms[1] = mean_second[0, 0]
        both = jnp.sqrt((mean_first + 1e-06) * (mean_second + 1e-06))
        for which in range(2):
            intersection[which] = (mean(1, which) / both)[0, 0]
        factor[...] = 1.0 / jnp.sqrt(mean_second + 1e-06)
        copy.wait()

    scale = factor[...]

    def group(i, carry):
        base = pl.multiple_of(i * (SUB * SUB), SUB * SUB)
        high = back[SUB + at * groups + i]
        for r in range(SUB):
            start = pl.multiple_of(high + back[r], SUB)
            for part in range(2):
                block = arrived[pl.ds(pl.multiple_of(start + part * part_rows, SUB), SUB), :]
                out[part, pl.ds(base + r, SUB, stride=SUB), :] = block * scale
        return carry

    lax.fori_loop(0, groups, group, 0, unroll=2)


def local(first_state, second_state, place_first, place_second):
    blocks_dev = first_state.shape[1]
    block = first_state.shape[2]
    wide_count = lax.axis_size("wide")
    narrow_count = lax.axis_size("narrow")
    devices = wide_count * narrow_count
    share = blocks_dev // devices
    lines = 1 + bits(blocks_dev * devices) - bits(LANE)

    def tiles(state):
        split = state.reshape(2, blocks_dev // SUB, SUB, block // LANE, LANE)
        return split.transpose(0, 1, 3, 2, 4).reshape(2 * blocks_dev * SUB, LANE)

    packed = (devices, 2, share, SUB, LANE)
    rows = (2 * blocks_dev * SUB, LANE)
    any_spec = pl.BlockSpec(memory_space=pl.ANY)
    smem_spec = pl.BlockSpec(memory_space=pltpu.SMEM)
    recv, stats, back = pl.pallas_call(
        functools.partial(exchange, (wide_count, narrow_count), blocks_dev, share),
        out_shape=(jax.ShapeDtypeStruct(packed, jnp.float32),
                   jax.ShapeDtypeStruct((2, 2, SUB, LANE), jnp.float32),
                   jax.ShapeDtypeStruct((SUB + blocks_dev // SUB,), jnp.int32)),
        in_specs=[any_spec] * 4,
        out_specs=(any_spec, pl.BlockSpec(memory_space=pltpu.VMEM), smem_spec),
        scratch_shapes=[
            pltpu.VMEM(rows, jnp.float32),
            pltpu.VMEM(rows, jnp.float32),
            pltpu.VMEM(packed, jnp.float32),
            pltpu.VMEM(packed, jnp.float32),
            pltpu.VMEM((2, 2, SUB, LANE), jnp.float32),
            pltpu.VMEM((2, devices, 2, SUB, LANE), jnp.float32),
            pltpu.SMEM((2, lines, LANE), jnp.int32),
            pltpu.SMEM((devices + share,), jnp.int32),
            pltpu.SMEM((devices + share,), jnp.int32),
            pltpu.SemaphoreType.DMA((2,)),
            pltpu.SemaphoreType.DMA((2 * lines,)),
        ] + [pltpu.SemaphoreType.DMA((devices,))] * 7,
        compiler_params=pltpu.CompilerParams(
            collective_id=0, has_side_effects=True, vmem_limit_bytes=48 * 1024 * 1024),
        name="exchange",
    )(place_first.reshape(-1, LANE), place_second.reshape(-1, LANE),
      tiles(first_state), tiles(second_state))

    steps = 8
    groups = blocks_dev // SUB // steps
    aligned, intersection, norms = pl.pallas_call(
        functools.partial(unpack, float(blocks_dev * devices * block), groups, share * SUB),
        out_shape=(jax.ShapeDtypeStruct((2, blocks_dev * SUB, LANE), jnp.float32),
                   jax.ShapeDtypeStruct((2,), jnp.float32),
                   jax.ShapeDtypeStruct((2,), jnp.float32)),
        grid=(steps,),
        in_specs=[smem_spec, pl.BlockSpec(memory_space=pltpu.VMEM), any_spec],
        out_specs=(pl.BlockSpec((2, groups * SUB * SUB, LANE), lambda i: (0, i, 0)), smem_spec, smem_spec),
        scratch_shapes=[pltpu.VMEM(rows, jnp.float32), pltpu.VMEM((SUB, LANE), jnp.float32),
                        pltpu.SemaphoreType.DMA],
        name="unpack",
    )(back, stats, recv.reshape(rows))
    aligned = aligned.reshape(2, blocks_dev // SUB, block // LANE, SUB, LANE)
    aligned = aligned.transpose(0, 1, 3, 2, 4).reshape(2, blocks_dev, block)
    return (aligned, intersection, norms)


def solution(mesh):
    return jax.shard_map(
        local,
        mesh=mesh,
        in_specs=(P(None, ("wide", "narrow"), None), P(None, ("wide", "narrow"), None), P(), P()),
        out_specs=(P(None, ("wide", "narrow"), None), P(), P()),
        check_vma=False,
    )
```

time: 512 us -> 222 us (0.43)
  between operations: 268 us -> 0.66 us
  Pallas kernels: 0 us -> 218 us
  local copies, waits for them, and re-layouts: 97.6 us -> 2.93 us
  other arithmetic: 73.7 us -> 0 us
  blocking collectives: 45.1 us -> 0 us
  waiting for transfers between devices: 15.4 us -> 0 us
  starting transfers between devices: 7.63 us -> 0 us
    pallas_call x0 -> x2, Pallas kernels: none -> 218 us  [the longest x1 208 us: local(): pl.pallas_call(functools.partial(exchange, (wide_count, narrow_count), bl...]
    gather x4 -> x0, local copies, waits for them, and re-layouts: 60.2 us -> none  [the longest x1 27.4 us: local(): outgoing = jnp.take(second_state, send_order, axis=1)]
    psum x1 -> x0, blocking collectives: 45.1 us -> none  [local(): lax.psum((first_sq, second_sq, real_part, imag_part), ('wide', 'narrow'))]
    reduce_sum x2 -> x0, other arithmetic: 38.5 us -> none  [the longest x1 30 us: local(): jnp.sum(first_state[0] * gathered[0] + first_state[1] * gathered[1])]
    all_to_all x1 -> x0, waiting for transfers between devices: 15.4 us -> none  [local(): lax.all_to_all(direct, ('wide', 'narrow'), split_axis=1, concat_axis=1, t...]
    all_to_all x1 -> x0, local copies, waits for them, and re-layouts: 15.3 us -> none  [local(): lax.all_to_all(direct, ('wide', 'narrow'), split_axis=1, concat_axis=1, t...]
    sort x3 -> x0, other arithmetic: 13.1 us -> none  [the longest x1 4.37 us: local(): send_order = jnp.argsort(target)]
    select_n x4 -> x0, other arithmetic: 12.5 us -> none  [the longest x1 8.33 us: local(): gathered = jnp.take(arrived, jnp.argsort(arrival_order), axis=1)]
  transfers between devices with their start and end apart: 1 -> 0, of which waited for: 1 -> 0; matrix products, arithmetic and copies ran while one was open for 7% -> 0% of each run, Pallas kernels for 0% -> 0%
where the time goes in v2:
time: 222 us; the launch traced here: 221 us
  Pallas kernels  218 us (98%)
  local copies, waits for them, and re-layouts  2.93 us (1%)
    pallas_call x1, Pallas kernels, local(): pl.pallas_call(functools.partial(exchange, (wide_count, narrow_count), bl...  208 us
    pallas_call x1, Pallas kernels, local(): pl.pallas_call(functools.partial(unpack, float(blocks_dev * devices * blo...  9.44 us

profile of v2, /device:TPU:0, one launch (start us, length us, event | category | flops | bytes accessed | tf_op | source)
XLA Modules:
  0.0 221.5 jit_solution(6577039447602529966)
XLA Ops:
  0.6 0.0 copy-start
  0.6 0.9 copy-done
  1.5 0.0 copy-start.1
  1.5 0.9 copy-done.1
  2.4 208.4 %exchange.1 = (f32[32,2,32,8,128]{4,3,2,1,0:T(8,128)}, f32[2,2,8,128]{3,2,1,0:T(8,128)S(1)}, s32[136]{0:T(256)S(1)}) custom-call(s32[256,128]{1,0:T(8,128)S(1)} %bitcast.18, s32[256,128]{1,0:T(8,128)S(1)} %bitcast.19, f32[16384,128]{1,0:T(8,128)} %bitcast.20, f32[16384,128]{1,0:T(8,128)} %bitcast.21), custom_call_target="tpu_custom_call" | custom-call | tf_op jit(solution)/shard_map/exchange/pallas_call | solution.py:307
  210.9 0.0 copy-start.2
  210.9 0.6 copy-done.2
  211.5 0.0 copy-start.3
  211.5 0.5 copy-done.3
  212.0 9.4 %unpack.1 = (f32[2,8192,128]{2,1,0:T(8,128)}, f32[2]{0:T(128)}, f32[2]{0:T(128)}) custom-call(s32[136]{0:T(256)} %copy-done.3, f32[2,2,8,128]{3,2,1,0:T(8,128)} %copy-done.2, f32[16384,128]{1,0:T(8,128)} %bitcast.22), custom_call_target="tpu_custom_call" | custom-call | tf_op jit(solution)/shard_map/unpack/pallas_call | solution.py:335
Async XLA Ops:
  0.6 0.9 copy-start
  1.5 0.9 copy-start.1
  210.9 0.6 copy-start.2
  211.5 0.5 copy-start.3
